TPU v7x, 128 devices: a whole 4x4x4 slice. The times are simulated.
128 devices in a mesh: seq: 8 (over x, core), tp: 16 (over y, z).
Axes of the slice: x: 4, y: 4, z: 4, core: 2. Of those that a mesh axis runs over, the one named last changes fastest.
Arguments:
- vit_input: bfloat16 [8192, 1280], P(('seq', 'tp')), may hold values from -6 to 6
- image_lengths: int32 [8, 2], P('seq'), may hold values from 1 to 192, 256 in all within a row
- positions: int32 [2048], replicated, may hold values from 0 to 2047, each once
- vit_ln_gain: float32 [1280], replicated, may hold values from 0.25 to 1.75
- w_qkv: bfloat16 [1280, 3, 1280], P(None, None, 'tp'), may hold values from -0.15625 to 0.15625
- w_proj: bfloat16 [1280, 1280], P('tp'), may hold values from -0.15625 to 0.15625
- merger_ln_gain: float32 [1280], replicated, may hold values from 0.25 to 1.75
- merger_w1: bfloat16 [5120, 5120], P(None, 'tp'), may hold values from -0.078125 to 0.078125
- merger_w2: bfloat16 [5120, 8192], P('tp'), may hold values from -0.36336105 to 0.36336105
- norm_gain: float32 [8192], P('seq'), may hold values from 0.25 to 1.75
- gate_up_weight: bfloat16 [8192, 2, 29568], P('seq', None, 'tp'), may hold values from -0.0625 to 0.0625
- down_weight: bfloat16 [29568, 8192], P('tp', 'seq'), may hold values from -0.125 to 0.125
Outputs:
- mixed: bfloat16 [2048, 8192], P('tp', 'seq')
Inputs may be any that keep to these rules, and one draw needn't show every extreme that they name: `image_lengths`: each row sums to 256. `positions`: a permutation: every slot once.
All inputs are finite; a program needn't handle non-finite values.
Results may differ from a plain program's by a relative error of at most 0.038.
Values may be sent and summed in bfloat16 or wider, within the bound.
A program may use at most 128 MiB of HBM per device.

v0:
```python
import jax
import jax.numpy as jnp
from jax import lax
from jax.sharding import Mesh
from jax.sharding import PartitionSpec as P

D = 8192
HD = 80
TP = ("tp_0", "tp_1")
SEQ_TP = ("seq", "tp_0", "tp_1")


def from_everyone(x, axis):
    copies = jnp.broadcast_to(x, (lax.axis_size(axis), *x.shape))
    return lax.all_to_all(copies, axis, split_axis=0, concat_axis=0, tiled=True)


def laid_out(tiles, dim):
    shape = list(tiles.shape[1:])
    shape[dim] *= tiles.shape[0]
    return jnp.moveaxis(tiles, 0, dim).reshape(shape)


def gathered_copies(x, axis, dim):
    tiles = from_everyone(x, axis)
    return laid_out(tiles, dim)


def cut_along(x, dim, devices):
    before, after = (x.shape[:dim], x.shape[dim + 1 :])
    return jnp.moveaxis(x.reshape(*before, devices, -1, *after), dim, 0)


def sum_at_owner(x, axis, dim):
    devices = lax.axis_size(axis)
    tiles = lax.all_to_all(cut_along(x, dim, devices), axis, 0, 0, tiled=True)
    return jnp.sum(tiles.astype(jnp.float32), axis=0)


def over_copies(x, axis):
    everything = from_everyone(x, axis)
    return jnp.sum(everything, axis=0)


def sum_by_axis(x, axes, dim):
    if not axes:
        return x
    nearer = lax.psum_scatter(x, axes[0], scatter_dimension=dim, tiled=True)
    return sum_by_axis(nearer, axes[1:], dim)


def layer_norm(values, gain):
    mean = jnp.mean(values, axis=-1, keepdims=True)
    centered = values - mean
    variance = jnp.mean(centered * centered, axis=-1, keepdims=True)
    return centered * lax.rsqrt(variance + 1e-06) * gain


def image_ids(lengths, count):
    image_ends = jnp.cumsum(lengths) * 4
    patch_index = jnp.arange(count, dtype=jnp.int32)
    return jnp.sum((patch_index[:, None] >= image_ends[None, :]).astype(jnp.int32), axis=1)


def attend(query, keys, values, image_index):
    scores = jnp.einsum("qhe,khe->hqk", query, keys, preferred_element_type=jnp.float32) * HD ** (
        -0.5
    )
    same_image = image_index[:, None] == image_index[None, :]
    scores = jnp.where(same_image[None], scores, -1e30)
    top = jnp.max(scores, axis=-1, keepdims=True)
    expo = jnp.exp(scores - top)
    weights = (expo / jnp.sum(expo, axis=-1, keepdims=True)).astype(jnp.bfloat16)
    output = jnp.einsum("hqk,khe->qhe", weights, values, preferred_element_type=jnp.float32)
    return output.astype(jnp.bfloat16)


def slot_sources(positions):
    count = positions.shape[0]
    return jnp.zeros((count,), jnp.int32).at[positions].set(jnp.arange(count, dtype=jnp.int32))


def local(
    vit_input,
    image_lengths,
    positions,
    vit_ln_gain,
    w_qkv,
    w_proj,
    merger_ln_gain,
    merger_w1,
    merger_w2,
    norm_gain,
    gate_up_weight,
    down_weight,
):
    tp_size = lax.axis_size(TP)
    seq_size = lax.axis_size("seq")
    own_patches = vit_input.shape[0]
    patch_width = vit_input.shape[1]
    head_cols = w_qkv.shape[2]
    local_heads = head_cols // HD
    normed_patches = layer_norm(vit_input.astype(jnp.float32), vit_ln_gain).astype(jnp.bfloat16)
    w_qkv_flat = w_qkv.reshape(patch_width, 3 * head_cols)
    projected = jnp.dot(
        gathered_copies(normed_patches, TP, 0), w_qkv_flat, preferred_element_type=jnp.float32
    ).astype(jnp.bfloat16)
    group_patches = projected.shape[0]
    projected = projected.reshape(group_patches, 3, local_heads, HD)
    image_index = image_ids(image_lengths[0], group_patches)
    attended = attend(projected[:, 0], projected[:, 1], projected[:, 2], image_index).reshape(
        group_patches, head_cols
    )
    picked = attended
    attn_sum = sum_at_owner(
        jnp.dot(picked, w_proj, preferred_element_type=jnp.float32).astype(jnp.bfloat16), TP, 0
    )
    vit_out = vit_input.astype(jnp.float32) + attn_sum
    own_tokens = own_patches // 4
    merged_in = (
        layer_norm(vit_out, merger_ln_gain)
        .astype(jnp.bfloat16)
        .reshape(own_tokens, 4 * patch_width)
    )
    expanded = jax.nn.gelu(
        jnp.dot(gathered_copies(merged_in, TP, 0), merger_w1, preferred_element_type=jnp.float32),
        approximate=False,
    ).astype(jnp.bfloat16)
    picked = expanded
    vis_rows = sum_at_owner(
        jnp.dot(picked, merger_w2, preferred_element_type=jnp.float32).astype(jnp.bfloat16), TP, 0
    ).astype(jnp.bfloat16)
    blocks = lax.all_to_all(vis_rows, "seq", split_axis=1, concat_axis=0, tiled=True)
    gathered = lax.all_gather(blocks, TP, axis=0, tiled=True)
    col_width = gathered.shape[1]
    all_tokens = (
        gathered.reshape(tp_size, seq_size, own_tokens, col_width)
        .transpose(1, 0, 2, 3)
        .reshape(tp_size * seq_size * own_tokens, col_width)
    )
    seq_rows = all_tokens.shape[0]
    seq_tokens = jnp.take(all_tokens, slot_sources(positions), axis=0)
    token_values = seq_tokens.astype(jnp.float32)
    row_squares = over_copies(jnp.sum(token_values * token_values, axis=1), "seq")
    inverse_rms = lax.rsqrt(row_squares / D + 1e-06)
    normed = (token_values * inverse_rms[:, None] * norm_gain).astype(jnp.bfloat16)
    slice_width = seq_tokens.shape[1]
    hidden_width = gate_up_weight.shape[2]
    weight_flat = gate_up_weight.reshape(slice_width, 2 * hidden_width)
    out_rows = seq_rows // tp_size
    picked = normed
    gate_up = lax.psum_scatter(
        jnp.dot(picked, weight_flat, preferred_element_type=jnp.float32).astype(jnp.bfloat16),
        "seq",
        scatter_dimension=0,
        tiled=True,
    ).astype(jnp.float32)
    hidden = (jax.nn.silu(gate_up[:, :hidden_width]) * gate_up[:, hidden_width:]).astype(
        jnp.bfloat16
    )
    terms = jnp.dot(
        lax.all_gather(hidden, "seq", axis=0, tiled=True),
        down_weight,
        preferred_element_type=jnp.float32,
    )
    down_sum = sum_by_axis(terms.astype(jnp.bfloat16), TP, 0).astype(jnp.float32)
    residual = lax.dynamic_slice_in_dim(token_values, lax.axis_index(TP) * out_rows, out_rows, 0)
    return (residual + down_sum).astype(jnp.bfloat16)


def solution(mesh):
    finer = Mesh(mesh.devices.reshape(mesh.shape["seq"], 4, 4), ("seq", "tp_0", "tp_1"))
    in_specs = (
        P(SEQ_TP, None),
        P("seq", None),
        P(),
        P(),
        P(None, None, TP),
        P(TP, None),
        P(),
        P(None, TP),
        P(TP, None),
        P("seq"),
        P("seq", None, TP),
        P(TP, "seq"),
    )
    out_specs = P(TP, "seq")
    return jax.shard_map(local, mesh=finer, in_specs=in_specs, out_specs=out_specs, check_vma=False)
```

profile of v0, /device:TPU:0, one launch (start us, length us, event | category | flops | bytes accessed | tf_op | source)
XLA Modules:
  0.0 555.1 jit_solution(18318716780304703547)
XLA Ops:
  6.5 0.0 copy-start
  6.5 1.2 convert_reduce_fusion.1
  7.7 1.1 fusion.11
  8.9 0.0 copy-start.8
  8.9 1.0 fusion.13
  9.9 1.8 broadcast_in_dim.26
  11.7 8.2 %all-to-all-start = ((bf16[16,64,1280]{2,1,0:T(8,128)(2,1)}), bf16[16,64,1280]{2,1,0:T(8,128)(2,1)}, u32[]{:S(2)}, u32[]{:S(2)}) async-start(bf16[16,64,1280]{2,1,0:T(8,128)(2,1)} %broadcast_in_dim.26), calls=%async_computation | async-start | bytes 5242880 | tf_op jit(solution)/shard_map/all_to_all | solution.py:15
  19.9 0.0 all-gather.3.cloned.1.call-start
  20.0 0.0 copy-done.8
  20.0 0.2 reduce-window.8
  20.2 0.1 fusion.57
  20.3 36.8 %all-to-all-done = bf16[16,64,1280]{2,1,0:T(8,128)(2,1)} async-done(((bf16[16,64,1280]{2,1,0:T(8,128)(2,1)}), bf16[16,64,1280]{2,1,0:T(8,128)(2,1)}, u32[]{:S(2)}, u32[]{:S(2)}) %all-to-all-start) | async-done | bytes 2621472 | tf_op jit(solution)/shard_map/all_to_all | solution.py:15
  57.1 2.7 convolution_convert_fusion.4
  59.8 0.0 copy-start.9
  59.8 0.0 copy-start.6
  59.8 0.9 fusion.4
  60.7 0.0 copy-start.3
  60.7 0.0 copy-done.9
  60.7 1.9 copy-done.3
  62.6 1.0 fusion.3
  63.6 0.0 copy-done.6
  63.6 6.0 %convolution_convert_fusion.2 = bf16[1024,1280]{1,0:T(8,128)(2,1)} fusion(bf16[80,1280]{1,0:T(8,128)(2,1)S(1)} %copy-done.6, f32[1024,1024]{0,1:T(8,128)} %copy-done.3, f32[1024]{0:T(1024)S(1)} %fusion.3, f32[1024]{0:T(1024)S(1)} %get-tuple-element.5, s32[1024]{0:T(1024)S(1)} %fusion.57, bf16[1024,3,1,80]{0,3,1,2:T(8,128)(2,1)} %bitcast.64), kind=kOutput, calls=%fused_computation.14 | convolution fusion | flops 385171456 | bytes 7200768 | tf_op jit(solution)/shard_map/dot_general | solution.py:116
  69.6 37.0 %all_to_all.45 = bf16[16,64,1280]{2,1,0:T(8,128)(2,1)S(1)} all-to-all(bf16[16,64,1280]{2,1,0:T(8,128)(2,1)} %bitcast.55), channel_id=1, replica_groups=mesh['seq'=8,'tp_0'=4,'tp_1'=4] {'tp_0','tp_1'}, dimensions={0} | all-to-all | bytes 5242880 | tf_op jit(solution)/shard_map/all_to_all | solution.py:36
  106.6 0.4 convert_reduce_fusion
  107.0 0.0 copy-done.2
  107.0 0.1 fusion.56
  107.1 0.2 multiply_reduce_fusion.1
  107.4 0.0 copy-done.5
  107.4 0.1 multiply_convert_fusion.2
  107.5 0.8 reshape.148
  108.3 1.2 broadcast_in_dim.47
  109.5 35.3 %all_to_all.46 = bf16[16,16,5120]{2,1,0:T(8,128)(2,1)} all-to-all(bf16[16,16,5120]{2,1,0:T(8,128)(2,1)S(1)} %broadcast_in_dim.47), channel_id=1, replica_groups=mesh['seq'=8,'tp_0'=4,'tp_1'=4] {'tp_0','tp_1'}, dimensions={0} | all-to-all | bytes 5242880 | tf_op jit(solution)/shard_map/all_to_all | solution.py:15
  144.8 0.0 copy-done
  144.8 10.9 %convolution_convert_fusion.1 = bf16[256,8192]{1,0:T(8,128)(2,1)} fusion(bf16[320,8192]{1,0:T(8,128)(2,1)} %param.20, bf16[256,5120]{1,0:T(8,128)(2,1)} %bitcast.56, bf16[5120,320]{0,1:T(8,128)(2,1)S(1)} %copy-done), kind=kOutput, calls=%fused_computation.3 | convolution fusion | flops 2188460032 | bytes 15335424 | tf_op jit(solution)/shard_map/dot_general | solution.py:131
  155.7 51.6 %all_to_all.47 = bf16[16,16,8192]{2,1,0:T(8,128)(2,1)} all-to-all(bf16[16,16,8192]{2,1,0:T(8,128)(2,1)} %bitcast.54), channel_id=1, replica_groups=mesh['seq'=8,'tp_0'=4,'tp_1'=4] {'tp_0','tp_1'}, dimensions={0} | all-to-all | bytes 8388608 | tf_op jit(solution)/shard_map/all_to_all | solution.py:36
  207.3 2.9 reduce_sum.100
  210.2 11.7 %all_to_all.48 = bf16[16,8,1024]{2,0,1:T(8,128)(2,1)} all-to-all(bf16[16,8,1024]{2,0,1:T(8,128)(2,1)S(1)} %bitcast.59), channel_id=1, replica_groups=mesh['seq'=8,'tp_0'=4,'tp_1'=4] {'seq'}, dimensions={1} | all-to-all | bytes 524288 | tf_op jit(solution)/shard_map/all_to_all | solution.py:133
  221.9 0.0 all-gather.3.cloned.1.call-update
  222.0 0.0 reduce-scatter.4.cloned.1.call-start
  222.0 8.0 %scatter_custom_fusion = s32[2048]{0:T(1024)S(1)} fusion(s32[2048]{0:T(1024)S(1)} %compare_select_fusion.1, s32[2048]{0:T(1024)S(1)} %iota.7, s32[]{:T(128)} %constant.45.clone.1), kind=kCustom, calls=%fused_computation.97 | custom fusion | bytes 8196 | tf_op jit(solution)/shard_map/scatter | solution.py:80
  230.1 39.4 %all-gather.3.cloned.1.call-done = bf16[2048,1024]{1,0:T(8,128)(2,1)} async-done(((bf16[128,1024]{1,0:T(8,128)(2,1)}), bf16[2048,1024]{1,0:T(8,128)(2,1)}) %all-gather.3.cloned.1.call-update) | async-done | bytes 4194320 | tf_op jit(solution)/shard_map/all_gather | solution.py:134
  269.6 5.0 copy.21
  274.6 13.7 %gather_fusion = bf16[2048,1024]{1,0:T(8,128)(2,1)} fusion(bf16[2048,1024]{1,0:T(8,128)(2,1)} %bitcast.52, s32[2048]{0:T(1024)S(1)} %fusion.58), kind=kCustom, calls=%fused_computation | custom fusion | bytes 8396800 | tf_op jit(solution)/shard_map/jit(_take)/gather | solution.py:142
  288.2 3.1 multiply_reduce_fusion
  291.4 9.7 %all_to_all.49 = f32[8,1,2048]{2,1,0:T(1,128)S(1)} all-to-all(f32[8,1,2048]{2,1,0:T(1,128)S(1)} %broadcast_in_dim.50), channel_id=1, replica_groups=mesh['seq'=8,'tp_0'=4,'tp_1'=4] {'seq'}, dimensions={0} | all-to-all | bytes 131072 | tf_op jit(solution)/shard_map/all_to_all | solution.py:15
  301.1 0.1 reduce_sum.102
  301.1 22.3 %convolution_convert_fusion = bf16[2048,3696]{0,1:T(8,128)(2,1)} fusion(bf16[1024,3696]{0,1:T(8,128)(2,1)} %bitcast.60, f32[1024]{0:T(1024)S(1)} %copy-done.7, f32[2048]{0:T(1024)S(1)} %add_rsqrt_fusion, bf16[2048,1024]{1,0:T(8,128)(2,1)} %gather_fusion, pred[2048]{0:T(1024)(128)(4,1)S(1)} %compare_and_fusion), kind=kOutput, calls=%fused_computation.2 | convolution fusion | flops 15520202752 | bytes 26916864 | tf_op jit(solution)/shard_map/dot_general | solution.py:153
  323.5 0.0 reduce-scatter.4.cloned.1.call-update
  323.5 0.0 all-gather.5.cloned.1.call-start
  323.5 82.4 %reduce-scatter.4.cloned.1.call-done = bf16[256,3696]{0,1:T(8,128)(2,1)} async-done(((bf16[2048,3696]{0,1:T(8,128)(2,1)}), bf16[256,3696]{0,1:T(8,128)(2,1)}) %reduce-scatter.4.cloned.1.call-update) | async-done | bytes 1892368 | tf_op jit(solution)/shard_map/reduce_scatter | solution.py:152
  405.9 1.8 convert_element_type.83
  407.7 1.6 fusion.6
  409.3 0.0 all-gather.5.cloned.1.call-update
  409.3 0.0 reduce-scatter.6.cloned.1.call-start
  409.4 49.6 %all-gather.5.cloned.1.call-done = bf16[2048,1848]{0,1:T(8,128)(2,1)} async-done(((bf16[256,1848]{0,1:T(8,128)(2,1)}), bf16[2048,1848]{0,1:T(8,128)(2,1)}) %all-gather.5.cloned.1.call-update) | async-done | bytes 7569424 | tf_op jit(solution)/shard_map/all_gather | solution.py:162
  459.0 13.7 %convolution_convert_fusion.3 = bf16[2048,1024]{1,0:T(8,128)(2,1)} fusion(bf16[2048,1848]{0,1:T(8,128)(2,1)} %all-gather.5.cloned.1.call-done, bf16[1848,1024]{1,0:T(8,128)(2,1)} %param.23), kind=kOutput, calls=%fused_computation.15 | convolution fusion | flops 7753170944 | bytes 15548416 | tf_op jit(solution)/shard_map/dot_general | solution.py:161
  472.7 0.0 reduce-scatter.6.cloned.1.call-update
  472.7 0.0 reduce-scatter.8.cloned.1.call-start
  472.8 47.9 %reduce-scatter.6.cloned.1.call-done = bf16[512,1024]{1,0:T(8,128)(2,1)} async-done(((bf16[2048,1024]{1,0:T(8,128)(2,1)}), bf16[512,1024]{1,0:T(8,128)(2,1)}) %reduce-scatter.6.cloned.1.call-update) | async-done | bytes 1048592 | tf_op jit(solution)/shard_map/reduce_scatter | solution.py:48
  520.7 0.0 reduce-scatter.8.cloned.1.call-update
  520.7 0.0 copy-start.1
  520.8 5.3 fusion.95
  526.1 20.6 %reduce-scatter.8.cloned.1.call-done = bf16[128,1024]{1,0:T(8,128)(2,1)} async-done(((bf16[512,1024]{1,0:T(8,128)(2,1)}), bf16[128,1024]{1,0:T(8,128)(2,1)}) %reduce-scatter.8.cloned.1.call-update) | async-done | bytes 262160 | tf_op jit(solution)/shard_map/reduce_scatter | solution.py:48
  546.7 1.9 add_convert_fusion
  (19 shorter events, 0.1 us)
Async XLA Ops:
  6.5 138.2 %copy-start = (bf16[5120,320]{0,1:T(8,128)(2,1)S(1)}, bf16[5120,320]{0,1:T(8,128)(2,1)}, u32[]{:S(2)}) copy-start(bf16[5120,320]{0,1:T(8,128)(2,1)} %param.19) | copy-start | bytes 9830404
  8.9 11.1 %copy-start.8 = (s32[1,2]{1,0:T(1,128)S(1)}, s32[1,2]{1,0:T(1,128)}, u32[]{:S(2)}) copy-start(s32[1,2]{1,0:T(1,128)} %param.13) | copy-start | bytes 28
  11.7 45.3 %all-to-all-start = ((bf16[16,64,1280]{2,1,0:T(8,128)(2,1)}), bf16[16,64,1280]{2,1,0:T(8,128)(2,1)}, u32[]{:S(2)}, u32[]{:S(2)}) async-start(bf16[16,64,1280]{2,1,0:T(8,128)(2,1)} %broadcast_in_dim.26), calls=%async_computation | async-start | bytes 5242880 | tf_op jit(solution)/shard_map/all_to_all | solution.py:15
  19.9 249.6 %all-gather.3.cloned.1.call-start = ((), (), s32[]{:S(2)}) async-start(), calls=%async_computation.9 | async-start | bytes 4456448 | tf_op jit(solution)/shard_map/all_gather | solution.py:134
  59.8 0.9 copy-start.9
  59.8 3.8 copy-start.6
  60.7 1.9 copy-start.3
  69.6 37.4 %copy-start.2 = (bf16[64,1280]{1,0:T(8,128)(2,1)S(1)}, bf16[64,1280]{1,0:T(8,128)(2,1)}, u32[]{:S(2)}) copy-start(bf16[64,1280]{1,0:T(8,128)(2,1)} %param.12) | copy-start | bytes 491524
  69.6 37.7 %copy-start.5 = (f32[1280]{0:T(1024)S(1)}, f32[1280]{0:T(1024)}, u32[]{:S(2)}) copy-start(f32[1280]{0:T(1024)} %param.18) | copy-start | bytes 15364
  207.3 14.7 %copy-start.4 = (s32[2048]{0:T(1024)S(1)}, s32[2048]{0:T(1024)}, u32[]{:S(2)}) copy-start(s32[2048]{0:T(1024)} %param.14) | copy-start | bytes 24580
  222.0 184.0 %reduce-scatter.4.cloned.1.call-start = ((), (), s32[]{:S(2)}) async-start(), calls=%async_computation.10 | async-start | bytes 17031168 | tf_op jit(solution)/shard_map/reduce_scatter | solution.py:152
  288.2 12.9 %copy-start.7 = (f32[1024]{0:T(1024)S(1)}, f32[1024]{0:T(1024)}, u32[]{:S(2)}) copy-start(f32[1024]{0:T(1024)} %param.21) | copy-start | bytes 12292
  323.5 135.5 %all-gather.5.cloned.1.call-start = ((), (), s32[]{:S(2)}) async-start(), calls=%async_computation.11 | async-start | bytes 8515584 | tf_op jit(solution)/shard_map/all_gather | solution.py:162
  409.3 111.4 %reduce-scatter.6.cloned.1.call-start = ((), (), s32[]{:S(2)}) async-start(), calls=%async_computation.12 | async-start | bytes 5242880 | tf_op jit(solution)/shard_map/reduce_scatter | solution.py:48
  472.7 74.0 %reduce-scatter.8.cloned.1.call-start = ((), (), s32[]{:S(2)}) async-start(), calls=%async_computation.13 | async-start | bytes 1310720 | tf_op jit(solution)/shard_map/reduce_scatter | solution.py:48
  520.7 27.8 %copy-start.1 = (bf16[5120,320]{0,1:T(8,128)(2,1)S(1)}, bf16[5120,320]{0,1:T(8,128)(2,1)}, u32[]{:S(2)}) copy-start(bf16[5120,320]{0,1:T(8,128)(2,1)} %param.19) | copy-start | bytes 9830404
Sparse Core Ops, SparseCore 0:
  222.1 47.4 all-gather.2
  323.6 82.2 reduce-scatter.3
  409.4 49.4 all-gather.4
  472.9 47.8 reduce-scatter.5
  523.0 23.6 reduce-scatter.7
where the time goes:
time: 556 us; the launch traced here: 555 us
  waiting for transfers between devices  277 us (50%)
  blocking collectives  145 us (26%)
  matrix products  56.6 us (10%)
  local copies, waits for them, and re-layouts  32.5 us (6%)
  other arithmetic  22.1 us (4%)
  between operations  13.4 us (2%)
  starting transfers between devices  8.41 us (2%)
    all_to_all x2, blocking collectives, sum_at_owner(): tiles = lax.all_to_all(cut_along(x, dim, devices), axis, 0, 0, tiled=True)  88.6 us
    reduce_scatter x1, waiting for transfers between devices, local(): lax.psum_scatter(jnp.dot(picked, weight_flat, preferred_element_type=jnp....  82.4 us
    reduce_scatter x2, waiting for transfers between devices, sum_by_axis(): nearer = lax.psum_scatter(x, axes[0], scatter_dimension=dim, tiled=True)  68.6 us
    all_gather x1, waiting for transfers between devices, local(): lax.all_gather(hidden, 'seq', axis=0, tiled=True)  49.6 us
    all_to_all x2, blocking collectives, from_everyone(): return lax.all_to_all(copies, axis, split_axis=0, concat_axis=0, tiled=True)  45 us
    all_gather x1, waiting for transfers between devices, local(): gathered = lax.all_gather(blocks, TP, axis=0, tiled=True)  39.4 us
    all_to_all x1, waiting for transfers between devices, from_everyone(): return lax.all_to_all(copies, axis, split_axis=0, concat_axis=0, tiled=True)  36.8 us
    dot_general x1, matrix products, local(): jnp.dot(picked, weight_flat, preferred_element_type=jnp.float32)  22.3 us
  transfers between devices with their start and end apart: 6, of which 6 were waited for; matrix products, arithmetic and copies ran while one was open for 2% of the time, Pallas kernels for 0%

commit v1 on v0

--- a/solution.py
+++ b/solution.py
@@ -159,7 +159,9 @@
         jnp.bfloat16
     )
     terms = jnp.dot(
-        lax.all_gather(hidden, "seq", axis=0, tiled=True),
+        jnp.concatenate(
+            lax.all_to_all(jnp.stack([hidden] * lax.axis_size("seq")), "seq", 0, 0), axis=0
+        ),
         down_weight,
         preferred_element_type=jnp.float32,
     )

time: 556 us -> 597 us (1.074)
  blocking collectives: 145 us -> 234 us
  waiting for transfers between devices: 277 us -> 226 us
    all_to_all x0 -> x1, blocking collectives: none -> 88.4 us  [local(): lax.all_to_all(jnp.stack([hidden] * lax.axis_size('seq')), 'seq', 0, 0)]
    all_gather x1 -> x0, waiting for transfers between devices: 49.6 us -> none  [local(): lax.all_gather(hidden, 'seq', axis=0, tiled=True)]
  transfers between devices with their start and end apart: 6 -> 5, of which waited for: 6 -> 5; matrix products, arithmetic and copies ran while one was open for 2% -> 2% of each run, Pallas kernels for 0% -> 0%
where the time goes in v1:
time: 597 us; the launch traced here: 596 us
  blocking collectives  234 us (39%)
  waiting for transfers between devices  226 us (38%)
  matrix products  56.5 us (9%)
  local copies, waits for them, and re-layouts  37.1 us (6%)
  other arithmetic  21.1 us (4%)
  between operations  13.4 us (2%)
  starting transfers between devices  8.37 us (1%)
    all_to_all x2, blocking collectives, sum_at_owner(): tiles = lax.all_to_all(cut_along(x, dim, devices), axis, 0, 0, tiled=True)  88.6 us
    all_to_all x1, blocking collectives, local(): lax.all_to_all(jnp.stack([hidden] * lax.axis_size('seq')), 'seq', 0, 0)  88.4 us
    reduce_scatter x1, waiting for transfers between devices, local(): lax.psum_scatter(jnp.dot(picked, weight_flat, preferred_element_type=jnp....  82.4 us
    reduce_scatter x2, waiting for transfers between devices, sum_by_axis(): nearer = lax.psum_scatter(x, axes[0], scatter_dimension=dim, tiled=True)  67.5 us
    all_to_all x2, blocking collectives, from_everyone(): return lax.all_to_all(copies, axis, split_axis=0, concat_axis=0, tiled=True)  45 us
    all_gather x1, waiting for transfers between devices, local(): gathered = lax.all_gather(blocks, TP, axis=0, tiled=True)  39.4 us
    all_to_all x1, waiting for transfers between devices, from_everyone(): return lax.all_to_all(copies, axis, split_axis=0, concat_axis=0, tiled=True)  36.8 us
    dot_general x1, matrix products, local(): jnp.dot(picked, weight_flat, preferred_element_type=jnp.float32)  22.3 us
  transfers between devices with their start and end apart: 5, of which 5 were waited for; matrix products, arithmetic and copies ran while one was open for 2% of the time, Pallas kernels for 0%

profile of v1, /device:TPU:0, one launch (start us, length us, event | category | flops | bytes accessed | tf_op | source)
XLA Modules:
  0.0 596.4 jit_solution(11052768886036411921)
XLA Ops:
  6.5 0.0 copy-start
  6.5 1.2 convert_reduce_fusion.1
  7.7 1.1 fusion.11
  8.9 0.0 copy-start.8
  8.9 1.0 fusion.13
  9.9 1.8 broadcast_in_dim.26
  11.7 8.2 %all-to-all-start = ((bf16[16,64,1280]{2,1,0:T(8,128)(2,1)}), bf16[16,64,1280]{2,1,0:T(8,128)(2,1)}, u32[]{:S(2)}, u32[]{:S(2)}) async-start(bf16[16,64,1280]{2,1,0:T(8,128)(2,1)} %broadcast_in_dim.26), calls=%async_computation | async-start | bytes 5242880 | tf_op jit(solution)/shard_map/all_to_all | solution.py:15
  19.9 0.0 all-gather.2.cloned.1.call-start
  20.0 0.0 copy-done.8
  20.0 0.2 reduce-window.8
  20.2 0.1 fusion.57
  20.3 36.8 %all-to-all-done = bf16[16,64,1280]{2,1,0:T(8,128)(2,1)} async-done(((bf16[16,64,1280]{2,1,0:T(8,128)(2,1)}), bf16[16,64,1280]{2,1,0:T(8,128)(2,1)}, u32[]{:S(2)}, u32[]{:S(2)}) %all-to-all-start) | async-done | bytes 2621472 | tf_op jit(solution)/shard_map/all_to_all | solution.py:15
  57.1 2.7 convolution_convert_fusion.4
  59.8 0.0 copy-start.9
  59.8 0.0 copy-start.6
  59.8 0.9 fusion.4
  60.7 0.0 copy-start.3
  60.7 0.0 copy-done.9
  60.7 1.9 copy-done.3
  62.6 1.0 fusion.3
  63.6 0.0 copy-done.6
  63.6 6.0 %convolution_convert_fusion.2 = bf16[1024,1280]{1,0:T(8,128)(2,1)} fusion(bf16[80,1280]{1,0:T(8,128)(2,1)S(1)} %copy-done.6, f32[1024,1024]{0,1:T(8,128)} %copy-done.3, f32[1024]{0:T(1024)S(1)} %fusion.3, f32[1024]{0:T(1024)S(1)} %get-tuple-element.5, s32[1024]{0:T(1024)S(1)} %fusion.57, bf16[1024,3,1,80]{0,3,1,2:T(8,128)(2,1)} %bitcast.68), kind=kOutput, calls=%fused_computation.14 | convolution fusion | flops 385171456 | bytes 7200768 | tf_op jit(solution)/shard_map/dot_general | solution.py:116
  69.6 37.0 %all_to_all.50 = bf16[16,64,1280]{2,1,0:T(8,128)(2,1)S(1)} all-to-all(bf16[16,64,1280]{2,1,0:T(8,128)(2,1)} %bitcast.59), channel_id=1, replica_groups=mesh['seq'=8,'tp_0'=4,'tp_1'=4] {'tp_0','tp_1'}, dimensions={0} | all-to-all | bytes 5242880 | tf_op jit(solution)/shard_map/all_to_all | solution.py:36
  106.6 0.4 convert_reduce_fusion
  107.0 0.0 copy-done.2
  107.0 0.1 fusion.56
  107.1 0.2 multiply_reduce_fusion.1
  107.4 0.0 copy-done.5
  107.4 0.1 multiply_convert_fusion.2
  107.5 0.8 reshape.153
  108.3 1.2 broadcast_in_dim.47
  109.5 35.3 %all_to_all.51 = bf16[16,16,5120]{2,1,0:T(8,128)(2,1)} all-to-all(bf16[16,16,5120]{2,1,0:T(8,128)(2,1)S(1)} %broadcast_in_dim.47), channel_id=1, replica_groups=mesh['seq'=8,'tp_0'=4,'tp_1'=4] {'tp_0','tp_1'}, dimensions={0} | all-to-all | bytes 5242880 | tf_op jit(solution)/shard_map/all_to_all | solution.py:15
  144.8 0.0 copy-done
  144.8 10.9 %convolution_convert_fusion.1 = bf16[256,8192]{1,0:T(8,128)(2,1)} fusion(bf16[320,8192]{1,0:T(8,128)(2,1)} %param.20, bf16[256,5120]{1,0:T(8,128)(2,1)} %bitcast.60, bf16[5120,320]{0,1:T(8,128)(2,1)S(1)} %copy-done), kind=kOutput, calls=%fused_computation.3 | convolution fusion | flops 2188460032 | bytes 15335424 | tf_op jit(solution)/shard_map/dot_general | solution.py:131
  155.7 51.6 %all_to_all.52 = bf16[16,16,8192]{2,1,0:T(8,128)(2,1)} all-to-all(bf16[16,16,8192]{2,1,0:T(8,128)(2,1)} %bitcast.58), channel_id=1, replica_groups=mesh['seq'=8,'tp_0'=4,'tp_1'=4] {'tp_0','tp_1'}, dimensions={0} | all-to-all | bytes 8388608 | tf_op jit(solution)/shard_map/all_to_all | solution.py:36
  207.3 2.9 reduce_sum.100
  210.2 11.7 %all_to_all.53 = bf16[16,8,1024]{2,0,1:T(8,128)(2,1)} all-to-all(bf16[16,8,1024]{2,0,1:T(8,128)(2,1)S(1)} %bitcast.63), channel_id=1, replica_groups=mesh['seq'=8,'tp_0'=4,'tp_1'=4] {'seq'}, dimensions={1} | all-to-all | bytes 524288 | tf_op jit(solution)/shard_map/all_to_all | solution.py:133
  221.9 0.0 all-gather.2.cloned.1.call-update
  222.0 0.0 reduce-scatter.4.cloned.1.call-start
  222.0 8.0 %scatter_custom_fusion = s32[2048]{0:T(1024)S(1)} fusion(s32[2048]{0:T(1024)S(1)} %compare_select_fusion.1, s32[2048]{0:T(1024)S(1)} %iota.7, s32[]{:T(128)} %constant.45.clone.1), kind=kCustom, calls=%fused_computation.97 | custom fusion | bytes 8196 | tf_op jit(solution)/shard_map/scatter | solution.py:80
  230.1 39.4 %all-gather.2.cloned.1.call-done = bf16[2048,1024]{1,0:T(8,128)(2,1)} async-done(((bf16[128,1024]{1,0:T(8,128)(2,1)}), bf16[2048,1024]{1,0:T(8,128)(2,1)}) %all-gather.2.cloned.1.call-update) | async-done | bytes 4194320 | tf_op jit(solution)/shard_map/all_gather | solution.py:134
  269.6 5.0 copy.28
  274.6 13.7 %gather_fusion = bf16[2048,1024]{1,0:T(8,128)(2,1)} fusion(bf16[2048,1024]{1,0:T(8,128)(2,1)} %bitcast.54, s32[2048]{0:T(1024)S(1)} %fusion.58), kind=kCustom, calls=%fused_computation | custom fusion | bytes 8396800 | tf_op jit(solution)/shard_map/jit(_take)/gather | solution.py:142
  288.2 3.1 multiply_reduce_fusion
  291.4 9.7 %all_to_all.54 = f32[8,1,2048]{2,1,0:T(1,128)S(1)} all-to-all(f32[8,1,2048]{2,1,0:T(1,128)S(1)} %broadcast_in_dim.50), channel_id=1, replica_groups=mesh['seq'=8,'tp_0'=4,'tp_1'=4] {'seq'}, dimensions={0} | all-to-all | bytes 131072 | tf_op jit(solution)/shard_map/all_to_all | solution.py:15
  301.1 0.1 reduce_sum.102
  301.1 22.3 %convolution_convert_fusion = bf16[2048,3696]{0,1:T(8,128)(2,1)} fusion(bf16[1024,3696]{0,1:T(8,128)(2,1)} %bitcast.64, f32[1024]{0:T(1024)S(1)} %copy-done.7, f32[2048]{0:T(1024)S(1)} %add_rsqrt_fusion, bf16[2048,1024]{1,0:T(8,128)(2,1)} %gather_fusion, pred[2048]{0:T(1024)(128)(4,1)S(1)} %compare_and_fusion), kind=kOutput, calls=%fused_computation.2 | convolution fusion | flops 15520202752 | bytes 26916864 | tf_op jit(solution)/shard_map/dot_general | solution.py:153
  323.5 0.0 reduce-scatter.4.cloned.1.call-update
  323.5 0.0 reduce-scatter.6.cloned.1.call-start
  323.5 82.4 %reduce-scatter.4.cloned.1.call-done = bf16[256,3696]{0,1:T(8,128)(2,1)} async-done(((bf16[2048,3696]{0,1:T(8,128)(2,1)}), bf16[256,3696]{0,1:T(8,128)(2,1)}) %reduce-scatter.4.cloned.1.call-update) | async-done | bytes 1892368 | tf_op jit(solution)/shard_map/reduce_scatter | solution.py:152
  405.9 1.8 convert_element_type.83
  407.7 0.6 fusion.6
  408.3 0.5 stack.2
  408.8 88.4 %all_to_all.55 = bf16[8,256,1848]{1,2,0:T(8,128)(2,1)S(1)} all-to-all(bf16[8,256,1848]{1,2,0:T(8,128)(2,1)S(1)} %stack.2), channel_id=1, replica_groups=mesh['seq'=8,'tp_0'=4,'tp_1'=4] {'seq'}, dimensions={0} | all-to-all | bytes 15138816 | tf_op jit(solution)/shard_map/all_to_all | solution.py:163
  497.2 4.1 copy.33
  501.3 13.7 %convolution_convert_fusion.3 = bf16[2048,1024]{1,0:T(8,128)(2,1)} fusion(bf16[2048,1848]{0,1:T(8,128)(2,1)} %bitcast.56, bf16[1848,1024]{1,0:T(8,128)(2,1)} %param.23), kind=kOutput, calls=%fused_computation.15 | convolution fusion | flops 7753170944 | bytes 15548416 | tf_op jit(solution)/shard_map/dot_general | solution.py:161
  515.0 0.0 reduce-scatter.6.cloned.1.call-update
  515.1 0.0 reduce-scatter.8.cloned.1.call-start
  515.1 46.8 %reduce-scatter.6.cloned.1.call-done = bf16[512,1024]{1,0:T(8,128)(2,1)} async-done(((bf16[2048,1024]{1,0:T(8,128)(2,1)}), bf16[512,1024]{1,0:T(8,128)(2,1)}) %reduce-scatter.6.cloned.1.call-update) | async-done | bytes 1048592 | tf_op jit(solution)/shard_map/reduce_scatter | solution.py:48
  561.9 0.0 reduce-scatter.8.cloned.1.call-update
  562.0 0.0 copy-start.1
  562.0 5.3 fusion.95
  567.3 20.7 %reduce-scatter.8.cloned.1.call-done = bf16[128,1024]{1,0:T(8,128)(2,1)} async-done(((bf16[512,1024]{1,0:T(8,128)(2,1)}), bf16[128,1024]{1,0:T(8,128)(2,1)}) %reduce-scatter.8.cloned.1.call-update) | async-done | bytes 262160 | tf_op jit(solution)/shard_map/reduce_scatter | solution.py:48
  588.0 1.9 add_convert_fusion
  (19 shorter events, 0.1 us)
Async XLA Ops:
  6.5 138.2 %copy-start = (bf16[5120,320]{0,1:T(8,128)(2,1)S(1)}, bf16[5120,320]{0,1:T(8,128)(2,1)}, u32[]{:S(2)}) copy-start(bf16[5120,320]{0,1:T(8,128)(2,1)} %param.19) | copy-start | bytes 9830404
  8.9 11.1 %copy-start.8 = (s32[1,2]{1,0:T(1,128)S(1)}, s32[1,2]{1,0:T(1,128)}, u32[]{:S(2)}) copy-start(s32[1,2]{1,0:T(1,128)} %param.13) | copy-start | bytes 28
  11.7 45.3 %all-to-all-start = ((bf16[16,64,1280]{2,1,0:T(8,128)(2,1)}), bf16[16,64,1280]{2,1,0:T(8,128)(2,1)}, u32[]{:S(2)}, u32[]{:S(2)}) async-start(bf16[16,64,1280]{2,1,0:T(8,128)(2,1)} %broadcast_in_dim.26), calls=%async_computation | async-start | bytes 5242880 | tf_op jit(solution)/shard_map/all_to_all | solution.py:15
  19.9 249.6 %all-gather.2.cloned.1.call-start = ((), (), s32[]{:S(2)}) async-start(), calls=%async_computation.10 | async-start | bytes 4456448 | tf_op jit(solution)/shard_map/all_gather | solution.py:134
  59.8 0.9 copy-start.9
  59.8 3.8 copy-start.6
  60.7 1.9 copy-start.3
  69.6 37.4 %copy-start.2 = (bf16[64,1280]{1,0:T(8,128)(2,1)S(1)}, bf16[64,1280]{1,0:T(8,128)(2,1)}, u32[]{:S(2)}) copy-start(bf16[64,1280]{1,0:T(8,128)(2,1)} %param.12) | copy-start | bytes 491524
  69.6 37.7 %copy-start.5 = (f32[1280]{0:T(1024)S(1)}, f32[1280]{0:T(1024)}, u32[]{:S(2)}) copy-start(f32[1280]{0:T(1024)} %param.18) | copy-start | bytes 15364
  207.3 14.7 %copy-start.4 = (s32[2048]{0:T(1024)S(1)}, s32[2048]{0:T(1024)}, u32[]{:S(2)}) copy-start(s32[2048]{0:T(1024)} %param.14) | copy-start | bytes 24580
  222.0 184.0 %reduce-scatter.4.cloned.1.call-start = ((), (), s32[]{:S(2)}) async-start(), calls=%async_computation.11 | async-start | bytes 17031168 | tf_op jit(solution)/shard_map/reduce_scatter | solution.py:152
  288.2 12.9 %copy-start.7 = (f32[1024]{0:T(1024)S(1)}, f32[1024]{0:T(1024)}, u32[]{:S(2)}) copy-start(f32[1024]{0:T(1024)} %param.21) | copy-start | bytes 12292
  323.5 238.4 %reduce-scatter.6.cloned.1.call-start = ((), (), s32[]{:S(2)}) async-start(), calls=%async_computation.12 | async-start | bytes 5242880 | tf_op jit(solution)/shard_map/reduce_scatter | solution.py:48
  515.1 72.9 %reduce-scatter.8.cloned.1.call-start = ((), (), s32[]{:S(2)}) async-start(), calls=%async_computation.13 | async-start | bytes 1310720 | tf_op jit(solution)/shard_map/reduce_scatter | solution.py:48
  562.0 27.9 %copy-start.1 = (bf16[5120,320]{0,1:T(8,128)(2,1)S(1)}, bf16[5120,320]{0,1:T(8,128)(2,1)}, u32[]{:S(2)}) copy-start(bf16[5120,320]{0,1:T(8,128)(2,1)} %param.19) | copy-start | bytes 9830404
Sparse Core Ops, SparseCore 0:
  222.1 47.4 all-gather.1
  323.6 82.2 reduce-scatter.3
  515.2 46.7 reduce-scatter.5
  564.2 23.7 reduce-scatter.7
